TPU v7x, 256 devices: a whole 4x4x8 slice. The times are simulated.
256 devices in a mesh: band: 64 (over y, z, core), feat: 4 (over x).
Axes of the slice: x: 4, y: 4, z: 8, core: 2. Of those that a mesh axis runs over, the one named last changes fastest.
Arguments:
- grid_latent: bfloat16 [131072, 512], P('band', 'feat'), may hold values from -6 to 6
- mesh_latent: bfloat16 [10240, 512], P('band', 'feat'), may hold values from -6 to 6
- edge_latent: bfloat16 [64, 4, 2048, 512], P('band', 'feat'), may hold values from -6 to 6
- edge_src: int32 [64, 8192], P('band'), may hold values from 0 to 2047
- edge_dst: int32 [64, 4, 2048], P('band', 'feat'), may hold values from 0 to 160, as said below
- edge_w1: bfloat16 [1536, 512], replicated, may hold values from -0.15625 to 0.15625
- edge_b1: float32 [512], replicated, may hold values from -3 to 3
- edge_w2: bfloat16 [512, 512], replicated, may hold values from -0.25 to 0.25
- edge_b2: float32 [512], replicated, may hold values from -2 to 2
- edge_gain: float32 [512], replicated, may hold values from 0.25 to 1.75
- edge_shift: float32 [512], replicated, may hold values from -2 to 2
- node_w1: bfloat16 [1024, 512], replicated, may hold values from -0.1875 to 0.1875
- node_b1: float32 [512], replicated, may hold values from -3 to 3
- node_w2: bfloat16 [512, 512], replicated, may hold values from -0.25 to 0.25
- node_b2: float32 [512], replicated, may hold values from -2 to 2
- node_gain: float32 [512], replicated, may hold values from 0.25 to 1.75
- node_shift: float32 [512], replicated, may hold values from -2 to 2
Outputs:
- mesh_new: bfloat16 [10240, 512], P('band', 'feat')
Inputs may be any that keep to these rules, and one draw needn't show every extreme that they name: `edge_src`: entry [s, d * 128 + j] is the grid row, counted within band index s, that sends slot j of the edges from band index s to band index d; empty slots hold some row too. `edge_dst`: entry [d, f, s * 32 + q] is the mesh node, counted within band index d, that receives slot f * 32 + q of the edges from band index s to band index d, or 160 where that slot is empty. The used slots of a pair come first; a pair has at most 128 used slots. Each receiving band index d hears only from the sending band indices of one latitude span of consecutive indices (edges are local), which lies anywhere along band since mesh partitions are face-major; other pairs are empty. In every draw some band indices receive 128 from every band index of their span.
All inputs are finite; a program needn't handle non-finite values.
Results may differ from a plain program's by a relative error of at most 0.011.
Values may be sent and summed in bfloat16 or wider, within the bound.
No kernel may reach another device: no remote copies, remote signals or barrier semaphores. Data moves between devices by JAX's collectives and lax.ppermute only.
A program may use at most 64 MiB of HBM per device.

v0:
```python
import math
import jax
import jax.numpy as jnp
from jax import lax
from jax.sharding import PartitionSpec as P

EPSILON = 1e-05


def cut_along(value, dim, length):
    shape = value.shape
    tiles = value.reshape(*shape[:dim], length, shape[dim] // length, *shape[dim + 1 :])
    return jnp.moveaxis(tiles, dim, 0)


def laid_out(tiles, dim):
    tiles = jnp.moveaxis(tiles, 0, dim)
    shape = tiles.shape
    return tiles.reshape(*shape[:dim], shape[dim] * shape[dim + 1], *shape[dim + 2 :])


def joined_exchange(value, axis, axes, splits, concats):
    sizes = [lax.axis_size(a) for a in axes]
    tiles = cut_along(value, splits[0], sizes[0])
    tiles = jnp.moveaxis(cut_along(tiles, splits[1] + 1, sizes[1]), 0, 1)
    inside = tiles.shape[2:]
    tiles = tiles.reshape(-1, *inside)
    tiles = lax.all_to_all(tiles, axis, split_axis=0, concat_axis=0, tiled=True)
    tiles = laid_out(tiles.reshape(*sizes, *inside), concats[0] + 1)
    return laid_out(tiles, concats[1])


def from_everyone(value, axis):
    length = lax.axis_size(axis)
    return lax.all_to_all(
        jnp.broadcast_to(value[None], (length, *value.shape)), axis, 0, 0, tiled=True
    )


def taken_together(value, axis):
    everything = from_everyone(value, axis)
    return jnp.sum(everything.astype(jnp.float32), axis=0)


def normalize(values, norm_gain, norm_shift):
    average = jnp.mean(values, -1, keepdims=True)
    centered = values - average
    variance = jnp.mean(centered * centered, -1, keepdims=True)
    return centered * lax.rsqrt(variance + EPSILON) * norm_gain + norm_shift


def node_step(row_block, summed, node_w1, node_b1, node_w2, node_b2, node_gain, node_shift):
    full_width = row_block.shape[1]
    hidden = jnp.dot(row_block, node_w1[:full_width], preferred_element_type=jnp.float32)
    hidden = (
        hidden
        + jnp.dot(
            summed.astype(jnp.bfloat16), node_w1[full_width:], preferred_element_type=jnp.float32
        )
        + node_b1
    )
    active = jax.nn.silu(hidden).astype(jnp.bfloat16)
    update = jnp.dot(active, node_w2, preferred_element_type=jnp.float32) + node_b2
    return (row_block.astype(jnp.float32) + normalize(update, node_gain, node_shift)).astype(
        jnp.bfloat16
    )


def select_rows(table, indices):
    total = indices.shape[0]
    block_rows = math.gcd(total, 512)
    grouped = indices.reshape(total // block_rows, block_rows)

    def one_block(block_ids):
        row_ids = lax.broadcasted_iota(jnp.int32, (block_rows, table.shape[0]), 1)
        onehot = (row_ids == block_ids[:, None]).astype(table.dtype)
        return jnp.dot(onehot, table, preferred_element_type=jnp.float32).astype(table.dtype)

    return lax.map(one_block, grouped).reshape(total, table.shape[1])


def body(
    grid_latent,
    mesh_latent,
    edge_latent,
    edge_src,
    edge_dst,
    edge_w1,
    edge_b1,
    edge_w2,
    edge_b2,
    edge_gain,
    edge_shift,
    node_w1,
    node_b1,
    node_w2,
    node_b2,
    node_gain,
    node_shift,
):
    band_count = lax.axis_size("band")
    feat_count = lax.axis_size("feat")
    quarter = grid_latent.shape[1]
    full_width = quarter * feat_count
    mesh_count = mesh_latent.shape[0]
    picked = select_rows(grid_latent, edge_src.reshape(-1)).reshape(band_count, -1, quarter)
    arrived = joined_exchange(picked, ("band", "feat"), ("band", "feat"), (0, 1), (0, 2))
    senders = arrived.reshape(-1, full_width)
    own_edges = edge_latent.reshape(-1, full_width)
    targets = edge_dst.reshape(-1)
    recv_weight = edge_w1[2 * full_width :]
    portion = lax.all_gather(mesh_latent, "feat", axis=1, tiled=True)
    projected = jnp.dot(portion, recv_weight, preferred_element_type=jnp.float32)
    node_ids = lax.broadcasted_iota(jnp.int32, (mesh_count, targets.shape[0]), 0)
    clipped = jnp.minimum(targets, mesh_count - 1)
    pick_node = (node_ids == clipped[None, :]).astype(jnp.float32)
    receiver_part = lax.dot_general(
        pick_node,
        projected,
        (((0,), (0,)), ((), ())),
        precision=lax.Precision.HIGHEST,
        preferred_element_type=jnp.float32,
    )
    hidden = jnp.dot(own_edges, edge_w1[:full_width], preferred_element_type=jnp.float32)
    hidden = hidden + jnp.dot(
        senders, edge_w1[full_width : 2 * full_width], preferred_element_type=jnp.float32
    )
    hidden = hidden + receiver_part + edge_b1
    active = jax.nn.silu(hidden).astype(jnp.bfloat16)
    update = jnp.dot(active, edge_w2, preferred_element_type=jnp.float32) + edge_b2
    edge_new = (own_edges.astype(jnp.float32) + normalize(update, edge_gain, edge_shift)).astype(
        jnp.bfloat16
    )
    selector = (node_ids == targets[None, :]).astype(jnp.bfloat16)
    partial_sums = jnp.dot(selector, edge_new, preferred_element_type=jnp.float32)
    summed = taken_together(partial_sums.astype(jnp.bfloat16), "feat").astype(jnp.float32)
    updated = node_step(portion, summed, node_w1, node_b1, node_w2, node_b2, node_gain, node_shift)
    own_cols = lax.dynamic_slice_in_dim(updated, lax.axis_index("feat") * quarter, quarter, 1)
    return own_cols


def solution(mesh):
    placed = (
        P("band", "feat"),
        P("band", "feat"),
        P("band", "feat", None, None),
        P("band", None),
        P("band", "feat", None),
        P(),
        P(),
        P(),
        P(),
        P(),
        P(),
        P(),
        P(),
        P(),
        P(),
        P(),
        P(),
    )
    return jax.shard_map(
        body, mesh=mesh, in_specs=placed, out_specs=P("band", "feat"), check_vma=False
    )
```

profile of v0, /device:TPU:1, one launch (start us, length us, event | category | flops | bytes accessed | tf_op | source)
XLA Modules:
  0.0 142.4 jit_solution(16497475571590522492)
XLA Ops:
  0.5 1.5 %reduce.4 = s32[8192]{0:T(1024)S(1)} reduce(s32[1,8192]{1,0:T(1,128)} %param.22, s32[]{:T(128)} %broadcast.66), dimensions={0}, to_apply=%param.22.reduce_sub_computation.3 | reduce | bytes 65540 | tf_op args[3]
  2.0 40.9 %while.10 = (s32[]{:T(128)}, bf16[16,512,128]{2,1,0:T(8,128)(2,1)}, s32[16,512]{1,0:T(8,128)S(1)}, bf16[2048,128]{1,0:T(8,128)(2,1)}, s32[]{:T(128)}) while((s32[]{:T(128)}, bf16[16,512,128]{2,1,0:T(8,128)(2,1)}, s32[16,512]{1,0:T(8,128)S(1)}, bf16[2048,128]{1,0:T(8,128)(2,1)}, s32[]{:T(128)}) %tuple.21), condition=%wide.region_1.2_spmd, body=%wide.region_0.1_spmd.sunk | while | flops 269549568 | bytes 662081 | solution.py:79
  2.0 2.5 %fusion.47 = bf16[16,512,128]{2,1,0:T(8,128)(2,1)} fusion(bf16[16,512,128]{2,1,0:T(8,128)(2,1)} %get-tuple-element.73, s32[]{:T(128)} %get-tuple-element.72, bf16[2048,128]{1,0:T(8,128)(2,1)} %get-tuple-element.80, s32[512]{0:T(512)S(1)} %bitcast.42), kind=kOutput, calls=%fused_computation.5.clone.1 | convolution fusion | flops 269549568 | bytes 657920 | tf_op jit(solution)/shard_map/while/body/eval_jaxpr/dot_general | solution.py:77
  4.6 2.5 %fusion.47 = bf16[16,512,128]{2,1,0:T(8,128)(2,1)} fusion(bf16[16,512,128]{2,1,0:T(8,128)(2,1)} %get-tuple-element.73, s32[]{:T(128)} %get-tuple-element.72, bf16[2048,128]{1,0:T(8,128)(2,1)} %get-tuple-element.80, s32[512]{0:T(512)S(1)} %bitcast.42), kind=kOutput, calls=%fused_computation.5.clone.1 | convolution fusion | flops 269549568 | bytes 657920 | tf_op jit(solution)/shard_map/while/body/eval_jaxpr/dot_general | solution.py:77
  7.1 2.5 %fusion.47 = bf16[16,512,128]{2,1,0:T(8,128)(2,1)} fusion(bf16[16,512,128]{2,1,0:T(8,128)(2,1)} %get-tuple-element.73, s32[]{:T(128)} %get-tuple-element.72, bf16[2048,128]{1,0:T(8,128)(2,1)} %get-tuple-element.80, s32[512]{0:T(512)S(1)} %bitcast.42), kind=kOutput, calls=%fused_computation.5.clone.1 | convolution fusion | flops 269549568 | bytes 657920 | tf_op jit(solution)/shard_map/while/body/eval_jaxpr/dot_general | solution.py:77
  9.7 2.6 %fusion.47 = bf16[16,512,128]{2,1,0:T(8,128)(2,1)} fusion(bf16[16,512,128]{2,1,0:T(8,128)(2,1)} %get-tuple-element.73, s32[]{:T(128)} %get-tuple-element.72, bf16[2048,128]{1,0:T(8,128)(2,1)} %get-tuple-element.80, s32[512]{0:T(512)S(1)} %bitcast.42), kind=kOutput, calls=%fused_computation.5.clone.1 | convolution fusion | flops 269549568 | bytes 657920 | tf_op jit(solution)/shard_map/while/body/eval_jaxpr/dot_general | solution.py:77
  12.3 2.5 %fusion.47 = bf16[16,512,128]{2,1,0:T(8,128)(2,1)} fusion(bf16[16,512,128]{2,1,0:T(8,128)(2,1)} %get-tuple-element.73, s32[]{:T(128)} %get-tuple-element.72, bf16[2048,128]{1,0:T(8,128)(2,1)} %get-tuple-element.80, s32[512]{0:T(512)S(1)} %bitcast.42), kind=kOutput, calls=%fused_computation.5.clone.1 | convolution fusion | flops 269549568 | bytes 657920 | tf_op jit(solution)/shard_map/while/body/eval_jaxpr/dot_general | solution.py:77
  14.8 2.5 %fusion.47 = bf16[16,512,128]{2,1,0:T(8,128)(2,1)} fusion(bf16[16,512,128]{2,1,0:T(8,128)(2,1)} %get-tuple-element.73, s32[]{:T(128)} %get-tuple-element.72, bf16[2048,128]{1,0:T(8,128)(2,1)} %get-tuple-element.80, s32[512]{0:T(512)S(1)} %bitcast.42), kind=kOutput, calls=%fused_computation.5.clone.1 | convolution fusion | flops 269549568 | bytes 657920 | tf_op jit(solution)/shard_map/while/body/eval_jaxpr/dot_general | solution.py:77
  17.4 2.5 %fusion.47 = bf16[16,512,128]{2,1,0:T(8,128)(2,1)} fusion(bf16[16,512,128]{2,1,0:T(8,128)(2,1)} %get-tuple-element.73, s32[]{:T(128)} %get-tuple-element.72, bf16[2048,128]{1,0:T(8,128)(2,1)} %get-tuple-element.80, s32[512]{0:T(512)S(1)} %bitcast.42), kind=kOutput, calls=%fused_computation.5.clone.1 | convolution fusion | flops 269549568 | bytes 657920 | tf_op jit(solution)/shard_map/while/body/eval_jaxpr/dot_general | solution.py:77
  19.9 2.5 %fusion.47 = bf16[16,512,128]{2,1,0:T(8,128)(2,1)} fusion(bf16[16,512,128]{2,1,0:T(8,128)(2,1)} %get-tuple-element.73, s32[]{:T(128)} %get-tuple-element.72, bf16[2048,128]{1,0:T(8,128)(2,1)} %get-tuple-element.80, s32[512]{0:T(512)S(1)} %bitcast.42), kind=kOutput, calls=%fused_computation.5.clone.1 | convolution fusion | flops 269549568 | bytes 657920 | tf_op jit(solution)/shard_map/while/body/eval_jaxpr/dot_general | solution.py:77
  22.5 2.5 %fusion.47 = bf16[16,512,128]{2,1,0:T(8,128)(2,1)} fusion(bf16[16,512,128]{2,1,0:T(8,128)(2,1)} %get-tuple-element.73, s32[]{:T(128)} %get-tuple-element.72, bf16[2048,128]{1,0:T(8,128)(2,1)} %get-tuple-element.80, s32[512]{0:T(512)S(1)} %bitcast.42), kind=kOutput, calls=%fused_computation.5.clone.1 | convolution fusion | flops 269549568 | bytes 657920 | tf_op jit(solution)/shard_map/while/body/eval_jaxpr/dot_general | solution.py:77
  25.0 2.5 %fusion.47 = bf16[16,512,128]{2,1,0:T(8,128)(2,1)} fusion(bf16[16,512,128]{2,1,0:T(8,128)(2,1)} %get-tuple-element.73, s32[]{:T(128)} %get-tuple-element.72, bf16[2048,128]{1,0:T(8,128)(2,1)} %get-tuple-element.80, s32[512]{0:T(512)S(1)} %bitcast.42), kind=kOutput, calls=%fused_computation.5.clone.1 | convolution fusion | flops 269549568 | bytes 657920 | tf_op jit(solution)/shard_map/while/body/eval_jaxpr/dot_general | solution.py:77
  27.6 2.5 %fusion.47 = bf16[16,512,128]{2,1,0:T(8,128)(2,1)} fusion(bf16[16,512,128]{2,1,0:T(8,128)(2,1)} %get-tuple-element.73, s32[]{:T(128)} %get-tuple-element.72, bf16[2048,128]{1,0:T(8,128)(2,1)} %get-tuple-element.80, s32[512]{0:T(512)S(1)} %bitcast.42), kind=kOutput, calls=%fused_computation.5.clone.1 | convolution fusion | flops 269549568 | bytes 657920 | tf_op jit(solution)/shard_map/while/body/eval_jaxpr/dot_general | solution.py:77
  30.1 2.5 %fusion.47 = bf16[16,512,128]{2,1,0:T(8,128)(2,1)} fusion(bf16[16,512,128]{2,1,0:T(8,128)(2,1)} %get-tuple-element.73, s32[]{:T(128)} %get-tuple-element.72, bf16[2048,128]{1,0:T(8,128)(2,1)} %get-tuple-element.80, s32[512]{0:T(512)S(1)} %bitcast.42), kind=kOutput, calls=%fused_computation.5.clone.1 | convolution fusion | flops 269549568 | bytes 657920 | tf_op jit(solution)/shard_map/while/body/eval_jaxpr/dot_general | solution.py:77
  32.7 2.5 %fusion.47 = bf16[16,512,128]{2,1,0:T(8,128)(2,1)} fusion(bf16[16,512,128]{2,1,0:T(8,128)(2,1)} %get-tuple-element.73, s32[]{:T(128)} %get-tuple-element.72, bf16[2048,128]{1,0:T(8,128)(2,1)} %get-tuple-element.80, s32[512]{0:T(512)S(1)} %bitcast.42), kind=kOutput, calls=%fused_computation.5.clone.1 | convolution fusion | flops 269549568 | bytes 657920 | tf_op jit(solution)/shard_map/while/body/eval_jaxpr/dot_general | solution.py:77
  35.2 2.5 %fusion.47 = bf16[16,512,128]{2,1,0:T(8,128)(2,1)} fusion(bf16[16,512,128]{2,1,0:T(8,128)(2,1)} %get-tuple-element.73, s32[]{:T(128)} %get-tuple-element.72, bf16[2048,128]{1,0:T(8,128)(2,1)} %get-tuple-element.80, s32[512]{0:T(512)S(1)} %bitcast.42), kind=kOutput, calls=%fused_computation.5.clone.1 | convolution fusion | flops 269549568 | bytes 657920 | tf_op jit(solution)/shard_map/while/body/eval_jaxpr/dot_general | solution.py:77
  37.8 2.5 %fusion.47 = bf16[16,512,128]{2,1,0:T(8,128)(2,1)} fusion(bf16[16,512,128]{2,1,0:T(8,128)(2,1)} %get-tuple-element.73, s32[]{:T(128)} %get-tuple-element.72, bf16[2048,128]{1,0:T(8,128)(2,1)} %get-tuple-element.80, s32[512]{0:T(512)S(1)} %bitcast.42), kind=kOutput, calls=%fused_computation.5.clone.1 | convolution fusion | flops 269549568 | bytes 657920 | tf_op jit(solution)/shard_map/while/body/eval_jaxpr/dot_general | solution.py:77
  40.3 2.5 %fusion.47 = bf16[16,512,128]{2,1,0:T(8,128)(2,1)} fusion(bf16[16,512,128]{2,1,0:T(8,128)(2,1)} %get-tuple-element.73, s32[]{:T(128)} %get-tuple-element.72, bf16[2048,128]{1,0:T(8,128)(2,1)} %get-tuple-element.80, s32[512]{0:T(512)S(1)} %bitcast.42), kind=kOutput, calls=%fused_computation.5.clone.1 | convolution fusion | flops 269549568 | bytes 657920 | tf_op jit(solution)/shard_map/while/body/eval_jaxpr/dot_general | solution.py:77
  42.9 16.6 %all-to-all-start = ((bf16[256,1,32,128]{3,2,1,0:T(8,128)(2,1)}), bf16[256,1,32,128]{3,2,1,0:T(8,128)(2,1)}, u32[]{:S(2)}, u32[]{:S(2)}) async-start(bf16[256,1,32,128]{3,2,1,0:T(8,128)(2,1)} %bitcast.4), calls=%async_computation | async-start | bytes 4194304 | tf_op jit(solution)/shard_map/all_to_all | solution.py:28
  59.5 2.5 %copy.24 = bf16[1,1,2048,512]{2,3,1,0:T(8,128)(2,1)} copy(bf16[1,1,2048,512]{3,2,1,0:T(8,128)(2,1)S(1)} %copy-done.1) | data formatting | bytes 4194304 | tf_op args[2]
  62.0 10.9 %all_gather.3 = bf16[160,512]{1,0:T(8,128)(2,1)S(1)} all-gather(bf16[160,128]{1,0:T(8,128)(2,1)S(1)} %copy-done.5), channel_id=1, replica_groups=mesh['band'=64,'feat'=4] {'feat'}, dimensions={1}, use_global_device_ids=true | all-gather | bytes 204800 | tf_op jit(solution)/shard_map/all_gather | solution.py:112
  72.9 1.3 fusion.16
  74.2 4.2 %fusion.8 = f32[2048,512]{1,0:T(8,128)} fusion(bf16[1,1,2048,512]{3,2,1,0:T(8,128)(2,1)S(1)} %copy-done.1, bf16[1536,512]{1,0:T(8,128)(2,1)} %param.24), kind=kOutput, calls=%fused_computation.14 | convolution fusion | flops 1073741824 | bytes 6815744 | tf_op jit(solution)/shard_map/dot_general | solution.py:124
  78.5 35.0 %all-to-all-done = bf16[256,1,32,128]{3,2,1,0:T(8,128)(2,1)} async-done(((bf16[256,1,32,128]{3,2,1,0:T(8,128)(2,1)}), bf16[256,1,32,128]{3,2,1,0:T(8,128)(2,1)}, u32[]{:S(2)}, u32[]{:S(2)}) %all-to-all-start) | async-done | bytes 2097184 | tf_op jit(solution)/shard_map/all_to_all | solution.py:28
  113.5 2.7 %copy.25 = bf16[64,32,4,128]{3,2,1,0:T(4,128)(2,1)S(1)} copy(bf16[64,32,4,128]{3,1,2,0:T(8,128)(2,1)} %bitcast.8) | data formatting | bytes 4194304 | tf_op jit(solution)/shard_map/transpose | solution.py:17
  116.2 2.4 %fusion.5 = f32[2048,512]{1,0:T(8,128)S(1)} fusion(bf16[256,8,4,128]{3,2,1,0:T(4,128)(2,1)S(1)} %bitcast.41, bf16[1536,512]{1,0:T(8,128)(2,1)} %param.24), kind=kOutput, calls=%fused_computation.11 | convolution fusion | flops 1073741824 | bytes 6815744 | tf_op jit(solution)/shard_map/dot_general | solution.py:125
  118.7 3.0 %multiply_convert_fusion = bf16[2048,512]{1,0:T(8,128)(2,1)S(1)} fusion(f32[2048,512]{1,0:T(8,128)S(1)} %copy-done.2, f32[2048,512]{1,0:T(8,128)S(1)} %fusion.5, f32[160,512]{1,0:T(8,128)S(1)} %fusion.16, f32[512]{0:T(512)S(1)} %copy-done.9, s32[2048]{0:T(1024)S(1)} %broadcast_minimum_fusion), kind=kOutput, calls=%fused_computation.9 | convolution fusion | flops 2021982208 | bytes 10823680 | tf_op jit(solution)/shard_map/dot_general | solution.py:117
  121.7 1.4 add_reduce_fusion
  123.8 0.9 copy-done.3
  124.7 1.6 %fusion.12 = bf16[160,512]{1,0:T(8,128)(2,1)S(1)} fusion(f32[2048,512]{0,1:T(8,128)S(1)} %get-tuple-element.39, bf16[1,1,2048,512]{2,3,1,0:T(8,128)(2,1)S(1)} %copy-done.3, f32[512]{0:T(512)S(1)} %copy-done.10, f32[512]{0:T(512)S(1)} %copy-done.11, f32[2048]{0:T(1024)S(1)} %add_rsqrt_fusion, f32[2048]{0:T(1024)S(1)} %broadcast_multiply_fusion, ...), kind=kOutput, calls=%fused_computation.22 | convolution fusion | flops 344342528 | bytes 6486016 | tf_op jit(solution)/shard_map/dot_general | solution.py:135
  127.2 3.5 %all-to-all-start.1 = ((bf16[4,160,512]{2,1,0:T(8,128)(2,1)}), bf16[4,160,512]{2,1,0:T(8,128)(2,1)S(1)}, u32[]{:S(2)}, u32[]{:S(2)}) async-start(bf16[4,160,512]{2,1,0:T(8,128)(2,1)} %broadcast_in_dim.10), calls=%async_computation.1 | async-start | bytes 1310720 | tf_op jit(solution)/shard_map/all_to_all | solution.py:35
  132.5 8.3 %all-to-all-done.1 = bf16[4,160,512]{2,1,0:T(8,128)(2,1)S(1)} async-done(((bf16[4,160,512]{2,1,0:T(8,128)(2,1)}), bf16[4,160,512]{2,1,0:T(8,128)(2,1)S(1)}, u32[]{:S(2)}, u32[]{:S(2)}) %all-to-all-start.1) | async-done | bytes 655392 | tf_op jit(solution)/shard_map/all_to_all | solution.py:35
  (60 shorter events, 5.6 us)
Async XLA Ops:
  0.0 121.7 %copy-start = (bf16[512,512]{1,0:T(8,128)(2,1)S(1)}, bf16[512,512]{1,0:T(8,128)(2,1)}, u32[]{:S(2)}) copy-start(bf16[512,512]{1,0:T(8,128)(2,1)} %param.26) | copy-start | bytes 1572868
  42.9 16.7 %copy-start.1 = (bf16[1,1,2048,512]{3,2,1,0:T(8,128)(2,1)S(1)}, bf16[1,1,2048,512]{3,2,1,0:T(8,128)(2,1)}, u32[]{:S(2)}) copy-start(bf16[1,1,2048,512]{3,2,1,0:T(8,128)(2,1)} %param.21) | copy-start | bytes 6291460
  42.9 19.2 %copy-start.5 = (bf16[160,128]{1,0:T(8,128)(2,1)S(1)}, bf16[160,128]{1,0:T(8,128)(2,1)}, u32[]{:S(2)}) copy-start(bf16[160,128]{1,0:T(8,128)(2,1)} %param.20) | copy-start | bytes 122884
  42.9 30.1 %copy-start.6 = (s32[1,1,2048]{2,1,0:T(1,128)S(1)}, s32[1,1,2048]{2,1,0:T(1,128)}, u32[]{:S(2)}) copy-start(s32[1,1,2048]{2,1,0:T(1,128)} %param.23) | copy-start | bytes 24580
  42.9 70.6 %all-to-all-start = ((bf16[256,1,32,128]{3,2,1,0:T(8,128)(2,1)}), bf16[256,1,32,128]{3,2,1,0:T(8,128)(2,1)}, u32[]{:S(2)}, u32[]{:S(2)}) async-start(bf16[256,1,32,128]{3,2,1,0:T(8,128)(2,1)} %bitcast.4), calls=%async_computation | async-start | bytes 4194304 | tf_op jit(solution)/shard_map/all_to_all | solution.py:28
  116.2 2.5 %copy-start.2 = (f32[2048,512]{1,0:T(8,128)S(1)}, f32[2048,512]{1,0:T(8,128)}, u32[]{:S(2)}) copy-start(f32[2048,512]{1,0:T(8,128)} %fusion.8) | copy-start | bytes 12582916
  116.2 2.5 %copy-start.9 = (f32[512]{0:T(512)S(1)}, f32[512]{0:T(512)}, u32[]{:S(2)}) copy-start(f32[512]{0:T(512)} %param.25) | copy-start | bytes 6148
  118.6 3.0 %copy-start.7 = (f32[512]{0:T(512)S(1)}, f32[512]{0:T(512)}, u32[]{:S(2)}) copy-start(f32[512]{0:T(512)} %param.27) | copy-start | bytes 6148
  123.1 1.6 %copy-start.3 = (bf16[1,1,2048,512]{2,3,1,0:T(8,128)(2,1)S(1)}, bf16[1,1,2048,512]{2,3,1,0:T(8,128)(2,1)}, u32[]{:S(2)}) copy-start(bf16[1,1,2048,512]{2,3,1,0:T(8,128)(2,1)} %copy.24) | copy-start | bytes 6291460
  123.1 1.6 %copy-start.10 = (f32[512]{0:T(512)S(1)}, f32[512]{0:T(512)}, u32[]{:S(2)}) copy-start(f32[512]{0:T(512)} %param.29) | copy-start | bytes 6148
  123.1 1.6 %copy-start.11 = (f32[512]{0:T(512)S(1)}, f32[512]{0:T(512)}, u32[]{:S(2)}) copy-start(f32[512]{0:T(512)} %param.28) | copy-start | bytes 6148
  124.7 7.6 %copy-start.4 = (bf16[1024,512]{1,0:T(8,128)(2,1)S(1)}, bf16[1024,512]{1,0:T(8,128)(2,1)}, u32[]{:S(2)}) copy-start(bf16[1024,512]{1,0:T(8,128)(2,1)} %param.30) | copy-start | bytes 3145732
  124.7 16.2 %copy-start.8 = (bf16[512,512]{1,0:T(8,128)(2,1)S(1)}, bf16[512,512]{1,0:T(8,128)(2,1)}, u32[]{:S(2)}) copy-start(bf16[512,512]{1,0:T(8,128)(2,1)} %param.32) | copy-start | bytes 1572868
  124.7 16.2 %copy-start.12 = (f32[512]{0:T(512)S(1)}, f32[512]{0:T(512)}, u32[]{:S(2)}) copy-start(f32[512]{0:T(512)} %param.33) | copy-start | bytes 6148
  124.7 16.2 %copy-start.13 = (f32[512]{0:T(512)S(1)}, f32[512]{0:T(512)}, u32[]{:S(2)}) copy-start(f32[512]{0:T(512)} %param.31) | copy-start | bytes 6148
  127.2 13.5 %all-to-all-start.1 = ((bf16[4,160,512]{2,1,0:T(8,128)(2,1)}), bf16[4,160,512]{2,1,0:T(8,128)(2,1)S(1)}, u32[]{:S(2)}, u32[]{:S(2)}) async-start(bf16[4,160,512]{2,1,0:T(8,128)(2,1)} %broadcast_in_dim.10), calls=%async_computation.1 | async-start | bytes 1310720 | tf_op jit(solution)/shard_map/all_to_all | solution.py:35
where the time goes:
time: 144 us; the launch traced here: 142 us
  matrix products  55.5 us (39%)
  waiting for transfers between devices  43.3 us (30%)
  starting transfers between devices  20.1 us (14%)
  blocking collectives  10.9 us (8%)
  local copies, waits for them, and re-layouts  9.17 us (6%)
  other arithmetic  3.13 us (2%)
    dot_general x16, matrix products, one_block(): jnp.dot(onehot, table, preferred_element_type=jnp.float32)  40.7 us
    all_to_all x1, waiting for transfers between devices, joined_exchange(): tiles = lax.all_to_all(tiles, axis, split_axis=0, concat_axis=0, tiled=True)  35 us
    all_to_all x1, starting transfers between devices, joined_exchange(): tiles = lax.all_to_all(tiles, axis, split_axis=0, concat_axis=0, tiled=True)  16.6 us
    all_gather x1, blocking collectives, body(): portion = lax.all_gather(mesh_latent, 'feat', axis=1, tiled=True)  10.9 us
    all_to_all x1, waiting for transfers between devices, from_everyone(): lax.all_to_all(jnp.broadcast_to(value[None], (length, *value.shape)), axi...  8.27 us
    dot_general x1, matrix products, body(): jnp.dot(own_edges, edge_w1[:full_width], preferred_element_type=jnp.float32)  4.24 us
    unnamed x30, local copies, waits for them, and re-layouts  3.98 us
    all_to_all x1, starting transfers between devices, from_everyone(): lax.all_to_all(jnp.broadcast_to(value[None], (length, *value.shape)), axi...  3.48 us
  transfers between devices with their start and end apart: 2, of which 2 were waited for; matrix products, arithmetic and copies ran while one was open for 7% of the time, Pallas kernels for 0%

commit v1 on v0

--- a/solution.py
+++ b/solution.py
@@ -109,7 +109,12 @@
     own_edges = edge_latent.reshape(-1, full_width)
     targets = edge_dst.reshape(-1)
     recv_weight = edge_w1[2 * full_width :]
-    portion = lax.all_gather(mesh_latent, "feat", axis=1, tiled=True)
+    ring = [mesh_latent]
+    for hop in range(3):
+        ring.append(lax.ppermute(ring[-1], "feat", [(dev, (dev + 1) % 4) for dev in range(4)]))
+    portion = jnp.roll(
+        jnp.concatenate(ring[::-1], axis=1), (lax.axis_index("feat") + 1) * ring[0].shape[1], axis=1
+    )
     projected = jnp.dot(portion, recv_weight, preferred_element_type=jnp.float32)
     node_ids = lax.broadcasted_iota(jnp.int32, (mesh_count, targets.shape[0]), 0)
     clipped = jnp.minimum(targets, mesh_count - 1)

time: 144 us -> 144 us (level)
  blocking collectives: 10.9 us -> 0 us
  waiting for transfers between devices: 43.3 us -> 52.1 us
  starting transfers between devices: 20.1 us -> 22.3 us
    all_gather x1 -> x0, blocking collectives: 10.9 us -> none  [body(): portion = lax.all_gather(mesh_latent, 'feat', axis=1, tiled=True)]
    ppermute x0 -> x3, waiting for transfers between devices: none -> 6.91 us  [body(): lax.ppermute(ring[-1], 'feat', [(dev, (dev + 1) % 4) for dev in range(4)])]
    ppermute x0 -> x3, starting transfers between devices: none -> 2.17 us  [body(): lax.ppermute(ring[-1], 'feat', [(dev, (dev + 1) % 4) for dev in range(4)])]
    all_to_all x1, waiting for transfers between devices: 35 us -> 36.6 us  [joined_exchange(): tiles = lax.all_to_all(tiles, axis, split_axis=0, concat_axis=0, tiled=True)]
    unnamed x30 -> x37, local copies, waits for them, and re-layouts: 3.98 us -> 4.05 us
  transfers between devices with their start and end apart: 2 -> 5, of which waited for: 2 -> 5; matrix products, arithmetic and copies ran while one was open for 7% -> 7% of each run, Pallas kernels for 0% -> 0%
where the time goes in v1:
time: 144 us; the launch traced here: 143 us
  matrix products  55.5 us (39%)
  waiting for transfers between devices  52.1 us (36%)
  starting transfers between devices  22.3 us (15%)
  local copies, waits for them, and re-layouts  9.25 us (6%)
  other arithmetic  3.08 us (2%)
    dot_general x16, matrix products, one_block(): jnp.dot(onehot, table, preferred_element_type=jnp.float32)  40.6 us
    all_to_all x1, waiting for transfers between devices, joined_exchange(): tiles = lax.all_to_all(tiles, axis, split_axis=0, concat_axis=0, tiled=True)  36.6 us
    all_to_all x1, starting transfers between devices, joined_exchange(): tiles = lax.all_to_all(tiles, axis, split_axis=0, concat_axis=0, tiled=True)  16.6 us
    all_to_all x1, waiting for transfers between devices, from_everyone(): lax.all_to_all(jnp.broadcast_to(value[None], (length, *value.shape)), axi...  8.54 us
    ppermute x3, waiting for transfers between devices, body(): lax.ppermute(ring[-1], 'feat', [(dev, (dev + 1) % 4) for dev in range(4)])  6.91 us
    dot_general x1, matrix products, body(): jnp.dot(own_edges, edge_w1[:full_width], preferred_element_type=jnp.float32)  4.23 us
    unnamed x37, local copies, waits for them, and re-layouts  4.05 us
    all_to_all x1, starting transfers between devices, from_everyone(): lax.all_to_all(jnp.broadcast_to(value[None], (length, *value.shape)), axi...  3.48 us
  transfers between devices with their start and end apart: 5, of which 5 were waited for; matrix products, arithmetic and copies ran while one was open for 7% of the time, Pallas kernels for 0%

profile of v1, /device:TPU:1, one launch (start us, length us, event | category | flops | bytes accessed | tf_op | source)
XLA Modules:
  0.0 142.6 jit_solution(1961370560749948848)
XLA Ops:
  0.5 1.4 reduce.4
  1.9 40.8 %while.10 = (s32[]{:T(128)}, bf16[16,512,128]{2,1,0:T(8,128)(2,1)}, s32[16,512]{1,0:T(8,128)S(1)}, bf16[2048,128]{1,0:T(8,128)(2,1)}, s32[]{:T(128)}) while((s32[]{:T(128)}, bf16[16,512,128]{2,1,0:T(8,128)(2,1)}, s32[16,512]{1,0:T(8,128)S(1)}, bf16[2048,128]{1,0:T(8,128)(2,1)}, s32[]{:T(128)}) %tuple.21), condition=%wide.region_1.2_spmd, body=%wide.region_0.1_spmd.sunk | while | flops 269549568 | bytes 662081 | solution.py:79
  1.9 2.5 %fusion.53 = bf16[16,512,128]{2,1,0:T(8,128)(2,1)} fusion(bf16[16,512,128]{2,1,0:T(8,128)(2,1)} %get-tuple-element.73, s32[]{:T(128)} %get-tuple-element.72, bf16[2048,128]{1,0:T(8,128)(2,1)} %get-tuple-element.80, s32[512]{0:T(512)S(1)} %bitcast.40), kind=kOutput, calls=%fused_computation.5.clone.1 | convolution fusion | flops 269549568 | bytes 657920 | tf_op jit(solution)/shard_map/while/body/eval_jaxpr/dot_general | solution.py:77
  4.5 2.5 %fusion.53 = bf16[16,512,128]{2,1,0:T(8,128)(2,1)} fusion(bf16[16,512,128]{2,1,0:T(8,128)(2,1)} %get-tuple-element.73, s32[]{:T(128)} %get-tuple-element.72, bf16[2048,128]{1,0:T(8,128)(2,1)} %get-tuple-element.80, s32[512]{0:T(512)S(1)} %bitcast.40), kind=kOutput, calls=%fused_computation.5.clone.1 | convolution fusion | flops 269549568 | bytes 657920 | tf_op jit(solution)/shard_map/while/body/eval_jaxpr/dot_general | solution.py:77
  7.1 2.5 %fusion.53 = bf16[16,512,128]{2,1,0:T(8,128)(2,1)} fusion(bf16[16,512,128]{2,1,0:T(8,128)(2,1)} %get-tuple-element.73, s32[]{:T(128)} %get-tuple-element.72, bf16[2048,128]{1,0:T(8,128)(2,1)} %get-tuple-element.80, s32[512]{0:T(512)S(1)} %bitcast.40), kind=kOutput, calls=%fused_computation.5.clone.1 | convolution fusion | flops 269549568 | bytes 657920 | tf_op jit(solution)/shard_map/while/body/eval_jaxpr/dot_general | solution.py:77
  9.6 2.5 %fusion.53 = bf16[16,512,128]{2,1,0:T(8,128)(2,1)} fusion(bf16[16,512,128]{2,1,0:T(8,128)(2,1)} %get-tuple-element.73, s32[]{:T(128)} %get-tuple-element.72, bf16[2048,128]{1,0:T(8,128)(2,1)} %get-tuple-element.80, s32[512]{0:T(512)S(1)} %bitcast.40), kind=kOutput, calls=%fused_computation.5.clone.1 | convolution fusion | flops 269549568 | bytes 657920 | tf_op jit(solution)/shard_map/while/body/eval_jaxpr/dot_general | solution.py:77
  12.1 2.5 %fusion.53 = bf16[16,512,128]{2,1,0:T(8,128)(2,1)} fusion(bf16[16,512,128]{2,1,0:T(8,128)(2,1)} %get-tuple-element.73, s32[]{:T(128)} %get-tuple-element.72, bf16[2048,128]{1,0:T(8,128)(2,1)} %get-tuple-element.80, s32[512]{0:T(512)S(1)} %bitcast.40), kind=kOutput, calls=%fused_computation.5.clone.1 | convolution fusion | flops 269549568 | bytes 657920 | tf_op jit(solution)/shard_map/while/body/eval_jaxpr/dot_general | solution.py:77
  14.7 2.5 %fusion.53 = bf16[16,512,128]{2,1,0:T(8,128)(2,1)} fusion(bf16[16,512,128]{2,1,0:T(8,128)(2,1)} %get-tuple-element.73, s32[]{:T(128)} %get-tuple-element.72, bf16[2048,128]{1,0:T(8,128)(2,1)} %get-tuple-element.80, s32[512]{0:T(512)S(1)} %bitcast.40), kind=kOutput, calls=%fused_computation.5.clone.1 | convolution fusion | flops 269549568 | bytes 657920 | tf_op jit(solution)/shard_map/while/body/eval_jaxpr/dot_general | solution.py:77
  17.2 2.5 %fusion.53 = bf16[16,512,128]{2,1,0:T(8,128)(2,1)} fusion(bf16[16,512,128]{2,1,0:T(8,128)(2,1)} %get-tuple-element.73, s32[]{:T(128)} %get-tuple-element.72, bf16[2048,128]{1,0:T(8,128)(2,1)} %get-tuple-element.80, s32[512]{0:T(512)S(1)} %bitcast.40), kind=kOutput, calls=%fused_computation.5.clone.1 | convolution fusion | flops 269549568 | bytes 657920 | tf_op jit(solution)/shard_map/while/body/eval_jaxpr/dot_general | solution.py:77
  19.8 2.5 %fusion.53 = bf16[16,512,128]{2,1,0:T(8,128)(2,1)} fusion(bf16[16,512,128]{2,1,0:T(8,128)(2,1)} %get-tuple-element.73, s32[]{:T(128)} %get-tuple-element.72, bf16[2048,128]{1,0:T(8,128)(2,1)} %get-tuple-element.80, s32[512]{0:T(512)S(1)} %bitcast.40), kind=kOutput, calls=%fused_computation.5.clone.1 | convolution fusion | flops 269549568 | bytes 657920 | tf_op jit(solution)/shard_map/while/body/eval_jaxpr/dot_general | solution.py:77
  22.3 2.5 %fusion.53 = bf16[16,512,128]{2,1,0:T(8,128)(2,1)} fusion(bf16[16,512,128]{2,1,0:T(8,128)(2,1)} %get-tuple-element.73, s32[]{:T(128)} %get-tuple-element.72, bf16[2048,128]{1,0:T(8,128)(2,1)} %get-tuple-element.80, s32[512]{0:T(512)S(1)} %bitcast.40), kind=kOutput, calls=%fused_computation.5.clone.1 | convolution fusion | flops 269549568 | bytes 657920 | tf_op jit(solution)/shard_map/while/body/eval_jaxpr/dot_general | solution.py:77
  24.9 2.5 %fusion.53 = bf16[16,512,128]{2,1,0:T(8,128)(2,1)} fusion(bf16[16,512,128]{2,1,0:T(8,128)(2,1)} %get-tuple-element.73, s32[]{:T(128)} %get-tuple-element.72, bf16[2048,128]{1,0:T(8,128)(2,1)} %get-tuple-element.80, s32[512]{0:T(512)S(1)} %bitcast.40), kind=kOutput, calls=%fused_computation.5.clone.1 | convolution fusion | flops 269549568 | bytes 657920 | tf_op jit(solution)/shard_map/while/body/eval_jaxpr/dot_general | solution.py:77
  27.4 2.5 %fusion.53 = bf16[16,512,128]{2,1,0:T(8,128)(2,1)} fusion(bf16[16,512,128]{2,1,0:T(8,128)(2,1)} %get-tuple-element.73, s32[]{:T(128)} %get-tuple-element.72, bf16[2048,128]{1,0:T(8,128)(2,1)} %get-tuple-element.80, s32[512]{0:T(512)S(1)} %bitcast.40), kind=kOutput, calls=%fused_computation.5.clone.1 | convolution fusion | flops 269549568 | bytes 657920 | tf_op jit(solution)/shard_map/while/body/eval_jaxpr/dot_general | solution.py:77
  30.0 2.5 %fusion.53 = bf16[16,512,128]{2,1,0:T(8,128)(2,1)} fusion(bf16[16,512,128]{2,1,0:T(8,128)(2,1)} %get-tuple-element.73, s32[]{:T(128)} %get-tuple-element.72, bf16[2048,128]{1,0:T(8,128)(2,1)} %get-tuple-element.80, s32[512]{0:T(512)S(1)} %bitcast.40), kind=kOutput, calls=%fused_computation.5.clone.1 | convolution fusion | flops 269549568 | bytes 657920 | tf_op jit(solution)/shard_map/while/body/eval_jaxpr/dot_general | solution.py:77
  32.5 2.5 %fusion.53 = bf16[16,512,128]{2,1,0:T(8,128)(2,1)} fusion(bf16[16,512,128]{2,1,0:T(8,128)(2,1)} %get-tuple-element.73, s32[]{:T(128)} %get-tuple-element.72, bf16[2048,128]{1,0:T(8,128)(2,1)} %get-tuple-element.80, s32[512]{0:T(512)S(1)} %bitcast.40), kind=kOutput, calls=%fused_computation.5.clone.1 | convolution fusion | flops 269549568 | bytes 657920 | tf_op jit(solution)/shard_map/while/body/eval_jaxpr/dot_general | solution.py:77
  35.0 2.5 %fusion.53 = bf16[16,512,128]{2,1,0:T(8,128)(2,1)} fusion(bf16[16,512,128]{2,1,0:T(8,128)(2,1)} %get-tuple-element.73, s32[]{:T(128)} %get-tuple-element.72, bf16[2048,128]{1,0:T(8,128)(2,1)} %get-tuple-element.80, s32[512]{0:T(512)S(1)} %bitcast.40), kind=kOutput, calls=%fused_computation.5.clone.1 | convolution fusion | flops 269549568 | bytes 657920 | tf_op jit(solution)/shard_map/while/body/eval_jaxpr/dot_general | solution.py:77
  37.6 2.6 %fusion.53 = bf16[16,512,128]{2,1,0:T(8,128)(2,1)} fusion(bf16[16,512,128]{2,1,0:T(8,128)(2,1)} %get-tuple-element.73, s32[]{:T(128)} %get-tuple-element.72, bf16[2048,128]{1,0:T(8,128)(2,1)} %get-tuple-element.80, s32[512]{0:T(512)S(1)} %bitcast.40), kind=kOutput, calls=%fused_computation.5.clone.1 | convolution fusion | flops 269549568 | bytes 657920 | tf_op jit(solution)/shard_map/while/body/eval_jaxpr/dot_general | solution.py:77
  40.1 2.5 %fusion.53 = bf16[16,512,128]{2,1,0:T(8,128)(2,1)} fusion(bf16[16,512,128]{2,1,0:T(8,128)(2,1)} %get-tuple-element.73, s32[]{:T(128)} %get-tuple-element.72, bf16[2048,128]{1,0:T(8,128)(2,1)} %get-tuple-element.80, s32[512]{0:T(512)S(1)} %bitcast.40), kind=kOutput, calls=%fused_computation.5.clone.1 | convolution fusion | flops 269549568 | bytes 657920 | tf_op jit(solution)/shard_map/while/body/eval_jaxpr/dot_general | solution.py:77
  42.7 16.6 %all-to-all-start = ((bf16[256,1,32,128]{3,2,1,0:T(8,128)(2,1)}), bf16[256,1,32,128]{3,2,1,0:T(8,128)(2,1)}, u32[]{:S(2)}, u32[]{:S(2)}) async-start(bf16[256,1,32,128]{3,2,1,0:T(8,128)(2,1)} %bitcast.4), calls=%async_computation | async-start | bytes 4194304 | tf_op jit(solution)/shard_map/all_to_all | solution.py:28
  59.4 1.4 %collective-permute-start = (bf16[160,128]{1,0:T(8,128)(2,1)S(1)}, bf16[160,128]{1,0:T(8,128)(2,1)S(1)}, u32[]{:S(2)}, u32[]{:S(2)}) collective-permute-start(bf16[160,128]{1,0:T(8,128)(2,1)S(1)} %copy-done.5), channel_id=1, source_target_pairs={{0,1},{1,2},{2,3},{3,0},{4,5},{5,6},{6,7},{7,4},{8,9},{9,10},{10,1... | collective-permute-start | bytes 122888 | tf_op jit(solution)/shard_map/ppermute | solution.py:114
  60.8 4.1 %collective-permute-done = bf16[160,128]{1,0:T(8,128)(2,1)S(1)} collective-permute-done((bf16[160,128]{1,0:T(8,128)(2,1)S(1)}, bf16[160,128]{1,0:T(8,128)(2,1)S(1)}, u32[]{:S(2)}, u32[]{:S(2)}) %collective-permute-start) | collective-permute-done | bytes 40992 | tf_op jit(solution)/shard_map/ppermute | solution.py:114
  65.1 4.2 %fusion.8 = f32[2048,512]{1,0:T(8,128)} fusion(bf16[1,1,2048,512]{3,2,1,0:T(8,128)(2,1)S(1)} %copy-done.1, bf16[1536,512]{1,0:T(8,128)(2,1)} %param.24), kind=kOutput, calls=%fused_computation.14 | convolution fusion | flops 1073741824 | bytes 6815744 | tf_op jit(solution)/shard_map/dot_general | solution.py:129
  70.5 2.5 %copy.24 = bf16[1,1,2048,512]{2,3,1,0:T(8,128)(2,1)} copy(bf16[1,1,2048,512]{3,2,1,0:T(8,128)(2,1)S(1)} %copy-done.1) | data formatting | bytes 4194304 | tf_op args[2]
  73.0 2.2 %collective-permute-done.2 = bf16[160,128]{1,0:T(8,128)(2,1)S(1)} collective-permute-done((bf16[160,128]{1,0:T(8,128)(2,1)S(1)}, bf16[160,128]{1,0:T(8,128)(2,1)S(1)}, u32[]{:S(2)}, u32[]{:S(2)}) %collective-permute-start.2) | collective-permute-done | bytes 40992 | tf_op jit(solution)/shard_map/ppermute | solution.py:114
  76.7 36.6 %all-to-all-done = bf16[256,1,32,128]{3,2,1,0:T(8,128)(2,1)} async-done(((bf16[256,1,32,128]{3,2,1,0:T(8,128)(2,1)}), bf16[256,1,32,128]{3,2,1,0:T(8,128)(2,1)}, u32[]{:S(2)}, u32[]{:S(2)}) %all-to-all-start) | async-done | bytes 2097184 | tf_op jit(solution)/shard_map/all_to_all | solution.py:28
  113.3 2.7 %copy.25 = bf16[64,32,4,128]{3,2,1,0:T(4,128)(2,1)S(1)} copy(bf16[64,32,4,128]{3,1,2,0:T(8,128)(2,1)} %bitcast.8) | data formatting | bytes 4194304 | tf_op jit(solution)/shard_map/transpose | solution.py:17
  116.0 2.5 %fusion.5 = f32[2048,512]{1,0:T(8,128)S(1)} fusion(bf16[256,8,4,128]{3,2,1,0:T(4,128)(2,1)S(1)} %bitcast.39, bf16[1536,512]{1,0:T(8,128)(2,1)} %param.24), kind=kOutput, calls=%fused_computation.11 | convolution fusion | flops 1073741824 | bytes 6815744 | tf_op jit(solution)/shard_map/dot_general | solution.py:130
  118.5 3.0 %multiply_convert_fusion = bf16[2048,512]{1,0:T(8,128)(2,1)S(1)} fusion(f32[2048,512]{1,0:T(8,128)S(1)} %copy-done.2, f32[2048,512]{1,0:T(8,128)S(1)} %fusion.5, f32[160,512]{1,0:T(8,128)S(1)} %fusion.17, f32[512]{0:T(512)S(1)} %copy-done.9, s32[2048]{0:T(1024)S(1)} %broadcast_minimum_fusion), kind=kOutput, calls=%fused_computation.9 | convolution fusion | flops 2021982208 | bytes 10823680 | tf_op jit(solution)/shard_map/dot_general | solution.py:122
  121.5 1.4 add_reduce_fusion
  124.5 1.6 %fusion.12 = bf16[160,512]{1,0:T(8,128)(2,1)S(1)} fusion(f32[2048,512]{0,1:T(8,128)S(1)} %get-tuple-element.39, bf16[1,1,2048,512]{2,3,1,0:T(8,128)(2,1)S(1)} %copy-done.3, f32[512]{0:T(512)S(1)} %copy-done.10, f32[512]{0:T(512)S(1)} %copy-done.11, f32[2048]{0:T(1024)S(1)} %add_rsqrt_fusion, f32[2048]{0:T(1024)S(1)} %broadcast_multiply_fusion, ...), kind=kOutput, calls=%fused_computation.22 | convolution fusion | flops 344342528 | bytes 6486016 | tf_op jit(solution)/shard_map/dot_general | solution.py:140
  127.1 3.5 %all-to-all-start.1 = ((bf16[4,160,512]{2,1,0:T(8,128)(2,1)}), bf16[4,160,512]{2,1,0:T(8,128)(2,1)S(1)}, u32[]{:S(2)}, u32[]{:S(2)}) async-start(bf16[4,160,512]{2,1,0:T(8,128)(2,1)} %broadcast_in_dim.10), calls=%async_computation.1 | async-start | bytes 1310720 | tf_op jit(solution)/shard_map/all_to_all | solution.py:35
  132.1 8.5 %all-to-all-done.1 = bf16[4,160,512]{2,1,0:T(8,128)(2,1)S(1)} async-done(((bf16[4,160,512]{2,1,0:T(8,128)(2,1)}), bf16[4,160,512]{2,1,0:T(8,128)(2,1)S(1)}, u32[]{:S(2)}, u32[]{:S(2)}) %all-to-all-start.1) | async-done | bytes 655392 | tf_op jit(solution)/shard_map/all_to_all | solution.py:35
  (73 shorter events, 9.4 us)
Async XLA Ops:
  0.0 121.5 %copy-start = (bf16[512,512]{1,0:T(8,128)(2,1)S(1)}, bf16[512,512]{1,0:T(8,128)(2,1)}, u32[]{:S(2)}) copy-start(bf16[512,512]{1,0:T(8,128)(2,1)} %param.26) | copy-start | bytes 1572868
  42.7 16.7 %copy-start.5 = (bf16[160,128]{1,0:T(8,128)(2,1)S(1)}, bf16[160,128]{1,0:T(8,128)(2,1)}, u32[]{:S(2)}) copy-start(bf16[160,128]{1,0:T(8,128)(2,1)} %param.20) | copy-start | bytes 122884
  42.7 22.4 %copy-start.1 = (bf16[1,1,2048,512]{3,2,1,0:T(8,128)(2,1)S(1)}, bf16[1,1,2048,512]{3,2,1,0:T(8,128)(2,1)}, u32[]{:S(2)}) copy-start(bf16[1,1,2048,512]{3,2,1,0:T(8,128)(2,1)} %param.21) | copy-start | bytes 6291460
  42.7 70.6 %all-to-all-start = ((bf16[256,1,32,128]{3,2,1,0:T(8,128)(2,1)}), bf16[256,1,32,128]{3,2,1,0:T(8,128)(2,1)}, u32[]{:S(2)}, u32[]{:S(2)}) async-start(bf16[256,1,32,128]{3,2,1,0:T(8,128)(2,1)} %bitcast.4), calls=%async_computation | async-start | bytes 4194304 | tf_op jit(solution)/shard_map/all_to_all | solution.py:28
  59.4 11.1 %copy-start.6 = (s32[1,1,2048]{2,1,0:T(1,128)S(1)}, s32[1,1,2048]{2,1,0:T(1,128)}, u32[]{:S(2)}) copy-start(s32[1,1,2048]{2,1,0:T(1,128)} %param.23) | copy-start | bytes 24580
  59.4 5.5 %collective-permute-start = (bf16[160,128]{1,0:T(8,128)(2,1)S(1)}, bf16[160,128]{1,0:T(8,128)(2,1)S(1)}, u32[]{:S(2)}, u32[]{:S(2)}) collective-permute-start(bf16[160,128]{1,0:T(8,128)(2,1)S(1)} %copy-done.5), channel_id=1, source_target_pairs={{0,1},{1,2},{2,3},{3,0},{4,5},{5,6},{6,7},{7,4},{8,9},{9,10},{10,1... | collective-permute-start | bytes 122888 | tf_op jit(solution)/shard_map/ppermute | solution.py:114
  64.9 5.1 %collective-permute-start.1 = (bf16[160,128]{1,0:T(8,128)(2,1)S(1)}, bf16[160,128]{1,0:T(8,128)(2,1)S(1)}, u32[]{:S(2)}, u32[]{:S(2)}) collective-permute-start(bf16[160,128]{1,0:T(8,128)(2,1)S(1)} %collective-permute-done), channel_id=1, source_target_pairs={{0,1},{1,2},{2,3},{3,0},{4,5},{5,6},{6,7},{7,4},{8,9},{9,10},{10,1... | collective-permute-start | bytes 122888 | tf_op jit(solution)/shard_map/ppermute | solution.py:114
  69.9 5.2 %collective-permute-start.2 = (bf16[160,128]{1,0:T(8,128)(2,1)S(1)}, bf16[160,128]{1,0:T(8,128)(2,1)S(1)}, u32[]{:S(2)}, u32[]{:S(2)}) collective-permute-start(bf16[160,128]{1,0:T(8,128)(2,1)S(1)} %collective-permute-done.1), channel_id=1, source_target_pairs={{0,1},{1,2},{2,3},{3,0},{4,5},{5,6},{6,7},{7,4},{8,9},{9,10},{10,1... | collective-permute-start | bytes 122888 | tf_op jit(solution)/shard_map/ppermute | solution.py:114
  116.0 2.5 %copy-start.2 = (f32[2048,512]{1,0:T(8,128)S(1)}, f32[2048,512]{1,0:T(8,128)}, u32[]{:S(2)}) copy-start(f32[2048,512]{1,0:T(8,128)} %fusion.8) | copy-start | bytes 12582916
  116.0 2.5 %copy-start.9 = (f32[512]{0:T(512)S(1)}, f32[512]{0:T(512)}, u32[]{:S(2)}) copy-start(f32[512]{0:T(512)} %param.25) | copy-start | bytes 6148
  118.5 3.0 %copy-start.7 = (f32[512]{0:T(512)S(1)}, f32[512]{0:T(512)}, u32[]{:S(2)}) copy-start(f32[512]{0:T(512)} %param.27) | copy-start | bytes 6148
  122.9 1.6 %copy-start.3 = (bf16[1,1,2048,512]{2,3,1,0:T(8,128)(2,1)S(1)}, bf16[1,1,2048,512]{2,3,1,0:T(8,128)(2,1)}, u32[]{:S(2)}) copy-start(bf16[1,1,2048,512]{2,3,1,0:T(8,128)(2,1)} %copy.24) | copy-start | bytes 6291460
  122.9 1.6 %copy-start.10 = (f32[512]{0:T(512)S(1)}, f32[512]{0:T(512)}, u32[]{:S(2)}) copy-start(f32[512]{0:T(512)} %param.29) | copy-start | bytes 6148
  122.9 1.6 %copy-start.11 = (f32[512]{0:T(512)S(1)}, f32[512]{0:T(512)}, u32[]{:S(2)}) copy-start(f32[512]{0:T(512)} %param.28) | copy-start | bytes 6148
  124.5 16.2 %copy-start.4 = (bf16[1024,512]{1,0:T(8,128)(2,1)S(1)}, bf16[1024,512]{1,0:T(8,128)(2,1)}, u32[]{:S(2)}) copy-start(bf16[1024,512]{1,0:T(8,128)(2,1)} %param.30) | copy-start | bytes 3145732
  124.5 16.4 %copy-start.8 = (bf16[512,512]{1,0:T(8,128)(2,1)S(1)}, bf16[512,512]{1,0:T(8,128)(2,1)}, u32[]{:S(2)}) copy-start(bf16[512,512]{1,0:T(8,128)(2,1)} %param.32) | copy-start | bytes 1572868
  124.5 16.5 %copy-start.12 = (f32[512]{0:T(512)S(1)}, f32[512]{0:T(512)}, u32[]{:S(2)}) copy-start(f32[512]{0:T(512)} %param.33) | copy-start | bytes 6148
  124.5 16.4 %copy-start.13 = (f32[512]{0:T(512)S(1)}, f32[512]{0:T(512)}, u32[]{:S(2)}) copy-start(f32[512]{0:T(512)} %param.31) | copy-start | bytes 6148
  127.1 13.5 %all-to-all-start.1 = ((bf16[4,160,512]{2,1,0:T(8,128)(2,1)}), bf16[4,160,512]{2,1,0:T(8,128)(2,1)S(1)}, u32[]{:S(2)}, u32[]{:S(2)}) async-start(bf16[4,160,512]{2,1,0:T(8,128)(2,1)} %broadcast_in_dim.10), calls=%async_computation.1 | async-start | bytes 1310720 | tf_op jit(solution)/shard_map/all_to_all | solution.py:35
